TPU v7x, 128 devices: a whole 4x4x4 slice. The times are simulated.
128 devices in a mesh: section: 32 (over y, z, core), tensor: 4 (over x).
Axes of the slice: x: 4, y: 4, z: 4, core: 2. Of those that a mesh axis runs over, the one named last changes fastest.
Arguments:
- section_input: bfloat16 [32, 512, 4096], P('section', 'tensor'), may hold values from -6 to 6
- history: bfloat16 [32, 7, 512, 4096], P('section', None, 'tensor'), may hold values from -6 to 6
- query_weight: bfloat16 [32, 4096, 3072], P('section', None, 'tensor'), may hold values from -0.4 to 0.4
- key_weight: bfloat16 [32, 4096, 512], P('section', None, 'tensor'), may hold values from -0.4 to 0.4
- value_weight: bfloat16 [32, 4096, 512], P('section', None, 'tensor'), may hold values from -0.09375 to 0.09375
- output_weight: bfloat16 [32, 3072, 4096], P('section', 'tensor'), may hold values from -0.5 to 0.5
- mix_weights: float32 [32, 8], replicated, may hold values from 0.2 to 0.6
Outputs:
- next_input: bfloat16 [32, 512, 4096], P('section', 'tensor')
All inputs are finite; a program needn't handle non-finite values.
Results may differ from a plain program's by a relative error of at most 0.013.
The roundings to bfloat16 on the way count: a program that leaves them out, or rounds other values in their place, can miss the bound.
Values may be sent and summed in bfloat16 or wider, within the bound.
No kernel may reach another device: no remote copies, remote signals or barrier semaphores. Data moves between devices by JAX's collectives and lax.ppermute only.
A program may use at most 128 MiB of HBM per device.

v0:
```python
import math
import jax
import jax.numpy as jnp
from jax import lax
from jax.sharding import PartitionSpec as P

HEAD_DIM = 64
DILATION_STRIDE = 4


def passed_along(value, axis, steps):
    count = lax.axis_size(axis)
    first, last = (max(0, -steps), min(count, count - steps))
    return lax.ppermute(value, axis, [(source, source + steps) for source in range(first, last)])


def from_behind(block, axis, distance):
    devices = range(lax.axis_size(axis))
    route = [((i - distance) % len(devices), i) for i in devices]
    return lax.ppermute(block, axis, route)


def normalize(token_rows):
    values = token_rows.astype(jnp.float32)
    inv_scale = lax.rsqrt(jnp.mean(values * values, axis=-1, keepdims=True) + 1e-05)
    return (values * inv_scale).astype(jnp.bfloat16)


def table_row(table, wanted):
    one_hot = (jnp.arange(table.shape[0], dtype=jnp.int32) == wanted).astype(jnp.float32)
    return jnp.sum(one_hot[:, None] * table, axis=0)


def attend(query_rows, key_rows, value_rows, first_row):
    scores = jnp.einsum(
        "tgjd,sgd->gjts", query_rows, key_rows, preferred_element_type=jnp.float32
    ) / math.sqrt(HEAD_DIM)
    row_positions = first_row + jnp.arange(query_rows.shape[0], dtype=jnp.int32)
    key_positions = jnp.arange(key_rows.shape[0], dtype=jnp.int32)
    scores = jnp.where(row_positions[:, None] >= key_positions[None, :], scores, -1e30)
    softmax_weights = jax.nn.softmax(scores, axis=-1).astype(jnp.bfloat16)
    heads_out = jnp.einsum(
        "gjts,sgd->tgjd", softmax_weights, value_rows, preferred_element_type=jnp.float32
    )
    return heads_out.astype(jnp.bfloat16)


def on_device(
    section_input, history, query_weight, key_weight, value_weight, output_weight, mix_weights
):
    token_rows = section_input[0]
    current_section = lax.axis_index("section")
    slots = history.shape[1]
    self_coefficient = table_row(mix_weights, current_section)
    history_sum = jnp.zeros(token_rows.shape, jnp.float32)
    for history_slot in range(1, slots + 1):
        received_block = passed_along(
            history[0, history_slot - 1], "section", DILATION_STRIDE * history_slot
        )
        factor = jnp.where(
            current_section >= DILATION_STRIDE * history_slot,
            self_coefficient[history_slot],
            jnp.float32(0.0),
        )
        history_sum = history_sum + factor * received_block.astype(jnp.float32)
    normed = normalize(token_rows)
    query_local = query_weight[0]
    key_local = key_weight[0]
    value_local = value_weight[0]
    row_piece = lax.all_gather(normed, "tensor", axis=0, tiled=True)
    query_part = jnp.dot(row_piece, query_local, preferred_element_type=jnp.float32).astype(
        jnp.bfloat16
    )
    key_part = jnp.dot(row_piece, key_local, preferred_element_type=jnp.float32).astype(
        jnp.bfloat16
    )
    value_part = jnp.dot(row_piece, value_local, preferred_element_type=jnp.float32).astype(
        jnp.bfloat16
    )
    projected = jnp.concatenate([query_part, key_part, value_part], axis=1)
    query_width = query_local.shape[1]
    kv_width = key_local.shape[1]
    seq_len = projected.shape[0]
    groups = kv_width // HEAD_DIM
    per_group = query_width // kv_width
    query_rows = projected[:, :query_width].reshape(seq_len, groups, per_group, HEAD_DIM)
    key_rows = projected[:, query_width : query_width + kv_width].reshape(seq_len, groups, HEAD_DIM)
    value_rows = projected[:, query_width + kv_width :].reshape(seq_len, groups, HEAD_DIM)
    block_rows = 512
    block_count = seq_len // block_rows
    blocked = query_rows.reshape(block_count, block_rows, groups, per_group, HEAD_DIM)
    starts = jnp.arange(block_count, dtype=jnp.int32) * block_rows
    attended = lax.map(
        lambda paired: attend(paired[0], key_rows, value_rows, paired[1]), (blocked, starts)
    )
    heads_out = attended.reshape(seq_len, query_width)
    output_local = output_weight[0]
    row_piece = heads_out
    partial_term = jnp.dot(row_piece, output_local, preferred_element_type=jnp.float32).astype(
        jnp.bfloat16
    )
    attention_sum = lax.psum_scatter(
        lax.optimization_barrier(partial_term).astype(jnp.float32).astype(jnp.bfloat16),
        "tensor",
        scatter_dimension=0,
        tiled=True,
    ).astype(jnp.float32)
    block_out = (token_rows.astype(jnp.float32) + attention_sum).astype(jnp.bfloat16)
    mixed = (self_coefficient[0] * block_out.astype(jnp.float32) + history_sum).astype(jnp.bfloat16)
    forwarded = from_behind(mixed, "section", 1)
    return forwarded[None]


def solution(mesh):
    placed = (
        P("section", "tensor", None),
        P("section", None, "tensor", None),
        P("section", None, "tensor"),
        P("section", None, "tensor"),
        P("section", None, "tensor"),
        P("section", "tensor", None),
        P(),
    )
    return jax.shard_map(
        on_device,
        mesh=mesh,
        in_specs=placed,
        out_specs=P("section", "tensor", None),
        check_vma=False,
    )
```

profile of v0, /device:TPU:0, one launch (start us, length us, event | category | flops | bytes accessed | tf_op | source)
XLA Modules:
  0.0 245.2 jit_solution(5167761586907813160)
XLA Ops:
  6.5 1.6 fusion.13
  8.2 2.5 %fusion.14 = bf16[128,4096]{1,0:T(8,128)(2,1)} fusion(bf16[1,128,4096]{2,1,0:T(8,128)(2,1)} %param.7, f32[128]{0:T(128)S(1)} %add_rsqrt_fusion), kind=kLoop, calls=%fused_computation.18 | loop fusion | flops 1572864 | bytes 2097664 | tf_op jit(solution)/shard_map/convert_element_type | solution.py:26
  10.8 50.7 %all-gather.2.cloned.1.call-done = bf16[512,4096]{1,0:T(8,128)(2,1)} async-done(((bf16[128,4096]{1,0:T(8,128)(2,1)}), bf16[512,4096]{1,0:T(8,128)(2,1)}) %all-gather.2.cloned.1.call-update) | async-done | bytes 4194320 | tf_op jit(solution)/shard_map/all_gather | solution.py:70
  61.5 7.5 %fusion.19 = bf16[512,768]{1,0:T(8,128)(2,1)S(1)} fusion(bf16[512,4096]{1,0:T(8,128)(2,1)} %all-gather.2.cloned.1.call-done, bf16[1,4096,768]{2,1,0:T(8,128)(2,1)} %param.9), kind=kOutput, calls=%fused_computation.23 | convolution fusion | flops 3221618688 | bytes 11272192 | tf_op jit(solution)/shard_map/dot_general | solution.py:71
  69.2 3.7 %convolution_convert_fusion = bf16[512,128]{0,1:T(8,128)(2,1)S(1)} fusion(bf16[512,4096]{1,0:T(8,128)(2,1)} %all-gather.2.cloned.1.call-done, bf16[1,4096,128]{2,1,0:T(8,128)(2,1)S(1)} %copy-done), kind=kOutput, calls=%fused_computation.24 | convolution fusion | flops 536936448 | bytes 5373952 | tf_op jit(solution)/shard_map/dot_general | solution.py:74
  72.9 7.3 %fusion.27 = (f32[2,6,512]{2,1,0:T(8,128)S(1)}, f32[2,6,512,512]{2,3,1,0:T(8,128)}) fusion(pred[512,512]{0,1:T(8,128)(4,1)S(1)} %iota_compare_fusion, bf16[512,2,64,1]{0,2,3,1:T(8,128)(2,1)S(1)} %bitcast.80, bf16[512,2,6,64]{0,3,2,1:T(8,128)(2,1)S(1)} %bitcast.79), kind=kOutput, calls=%fused_computation.42 | convolution fusion | flops 415236608 | bytes 13787136 | tf_op jit(solution)/shard_map/while/body/eval_jaxpr/sub | solution.py:41
  80.2 3.8 %convolution_convert_fusion.1 = bf16[512,128]{0,1:T(8,128)(2,1)S(1)} fusion(bf16[512,4096]{1,0:T(8,128)(2,1)} %all-gather.2.cloned.1.call-done, bf16[1,4096,128]{2,1,0:T(8,128)(2,1)S(1)} %copy-done.2), kind=kOutput, calls=%fused_computation.25 | convolution fusion | flops 536936448 | bytes 5373952 | tf_op jit(solution)/shard_map/dot_general | solution.py:77
  84.1 6.0 %fusion.18 = bf16[2,64,6,512]{3,1,2,0:T(8,128)(2,1)S(1)} fusion(bf16[512,2,64,1]{0,2,3,1:T(8,128)(2,1)S(1)} %bitcast.81, f32[2,6,512,512]{2,3,1,0:T(8,128)} %get-tuple-element.36, f32[2,6,512]{2,1,0:T(8,128)S(1)} %get-tuple-element.35), kind=kOutput, calls=%fused_computation.22 | convolution fusion | flops 409337856 | bytes 13524992 | tf_op jit(solution)/shard_map/while/body/eval_jaxpr/gjts,sgd->tgjd/dot_general | solution.py:42
  90.1 5.2 %fusion.10 = bf16[512,4096]{1,0:T(8,128)(2,1)} fusion(bf16[512,768]{0,1:T(8,128)(2,1)S(1)} %bitcast.84, bf16[1,768,4096]{2,1,0:T(8,128)(2,1)S(1)} %bitcast.83), kind=kOutput, calls=%fused_computation.13 | convolution fusion | flops 3223322624 | bytes 11272192 | tf_op jit(solution)/shard_map/dot_general | solution.py:99
  95.4 5.6 %slice_bitcast_fusion.6 = (bf16[128,4096]{1,0:T(8,128)(2,1)S(1)}, bf16[128,4096]{1,0:T(8,128)(2,1)}, bf16[128,4096]{1,0:T(8,128)(2,1)}, bf16[128,4096]{1,0:T(8,1...) fusion(bf16[1,7,128,4096]{3,2,1,0:T(8,128)(2,1)} %param.8), kind=kLoop, calls=%fused_computation.34 | loop fusion | bytes 14680064 | tf_op jit(solution)/shard_map/squeeze | solution.py:58
  100.9 5.1 %collective-permute-start = (bf16[128,4096]{1,0:T(8,128)(2,1)S(1)}, bf16[128,4096]{1,0:T(8,128)(2,1)S(1)}, u32[]{:S(2)}, u32[]{:S(2)}) collective-permute-start(bf16[128,4096]{1,0:T(8,128)(2,1)S(1)} %get-tuple-element.13), channel_id=1, source_target_pairs={{0,16},{4,20},{8,24},{12,28},{16,32},{20,36},{24,40},{28,44},{32,4... | collective-permute-start | bytes 3145736 | tf_op jit(solution)/shard_map/ppermute | solution.py:14
  106.1 3.4 %collective-permute-start.1 = (bf16[128,4096]{1,0:T(8,128)(2,1)S(1)}, bf16[128,4096]{1,0:T(8,128)(2,1)S(1)}, u32[]{:S(2)}, u32[]{:S(2)}) collective-permute-start(bf16[128,4096]{1,0:T(8,128)(2,1)S(1)} %get-tuple-element.24), channel_id=1, source_target_pairs={{0,32},{4,36},{8,40},{12,44},{16,48},{20,52},{24,56},{28,60},{32,6... | collective-permute-start | bytes 3145736 | tf_op jit(solution)/shard_map/ppermute | solution.py:14
  109.5 4.7 %collective-permute-start.2 = (bf16[128,4096]{1,0:T(8,128)(2,1)}, bf16[128,4096]{1,0:T(8,128)(2,1)}, u32[]{:S(2)}, u32[]{:S(2)}) collective-permute-start(bf16[128,4096]{1,0:T(8,128)(2,1)} %get-tuple-element.22), channel_id=1, source_target_pairs={{0,48},{4,52},{8,56},{12,60},{16,64},{20,68},{24,72},{28,76},{32,8... | collective-permute-start | bytes 3145736 | tf_op jit(solution)/shard_map/ppermute | solution.py:14
  114.2 2.8 %collective-permute-start.3 = (bf16[128,4096]{1,0:T(8,128)(2,1)}, bf16[128,4096]{1,0:T(8,128)(2,1)}, u32[]{:S(2)}, u32[]{:S(2)}) collective-permute-start(bf16[128,4096]{1,0:T(8,128)(2,1)} %get-tuple-element.20), channel_id=1, source_target_pairs={{0,64},{4,68},{8,72},{12,76},{16,80},{20,84},{24,88},{28,92},{32,9... | collective-permute-start | bytes 3145736 | tf_op jit(solution)/shard_map/ppermute | solution.py:14
  117.0 2.3 collective-permute-start.4
  119.3 8.9 %collective-permute-done = bf16[128,4096]{1,0:T(8,128)(2,1)S(1)} collective-permute-done((bf16[128,4096]{1,0:T(8,128)(2,1)S(1)}, bf16[128,4096]{1,0:T(8,128)(2,1)S(1)}, u32[]{:S(2)}, u32[]{:S(2)}) %collective-permute-start) | collective-permute-done | bytes 1048608 | tf_op jit(solution)/shard_map/ppermute | solution.py:14
  128.2 29.9 %collective-permute-start.5 = (bf16[128,4096]{1,0:T(8,128)(2,1)}, bf16[128,4096]{1,0:T(8,128)(2,1)}, u32[]{:S(2)}, u32[]{:S(2)}) collective-permute-start(bf16[128,4096]{1,0:T(8,128)(2,1)} %get-tuple-element.26), channel_id=1, source_target_pairs={{0,96},{4,100},{8,104},{12,108},{16,112},{20,116},{24,120},{28,124... | collective-permute-start | bytes 3145736 | tf_op jit(solution)/shard_map/ppermute | solution.py:14
  158.2 20.5 %collective-permute-start.6 = (bf16[128,4096]{1,0:T(8,128)(2,1)S(1)}, bf16[128,4096]{1,0:T(8,128)(2,1)}, u32[]{:S(2)}, u32[]{:S(2)}) collective-permute-start(bf16[128,4096]{1,0:T(8,128)(2,1)S(1)} %get-tuple-element.25), channel_id=1, source_target_pairs={{0,112},{4,116},{8,120},{12,124},{1,113},{5,117},{9,121},{13,125},... | collective-permute-start | bytes 3145736 | tf_op jit(solution)/shard_map/ppermute | solution.py:14
  178.8 0.7 fusion.26
  183.8 15.1 %collective-permute-done.4 = bf16[128,4096]{1,0:T(8,128)(2,1)} collective-permute-done((bf16[128,4096]{1,0:T(8,128)(2,1)}, bf16[128,4096]{1,0:T(8,128)(2,1)}, u32[]{:S(2)}, u32[]{:S(2)}) %collective-permute-start.4) | collective-permute-done | bytes 1048608 | tf_op jit(solution)/shard_map/ppermute | solution.py:14
  198.9 11.4 %collective-permute-done.6 = bf16[128,4096]{1,0:T(8,128)(2,1)} collective-permute-done((bf16[128,4096]{1,0:T(8,128)(2,1)S(1)}, bf16[128,4096]{1,0:T(8,128)(2,1)}, u32[]{:S(2)}, u32[]{:S(2)}) %collective-permute-start.6) | collective-permute-done | bytes 1048608 | tf_op jit(solution)/shard_map/ppermute | solution.py:14
  210.3 5.8 %add_convert_fusion = bf16[128,4096]{1,0:T(8,128)(2,1)S(1)} fusion(bf16[128,4096]{1,0:T(8,128)(2,1)} %collective-permute-done.6, bf16[128,4096]{1,0:T(8,128)(2,1)} %collective-permute-done.5, bf16[128,4096]{1,0:T(8,128)(2,1)} %collective-permute-done.4, bf16[128,4096]{1,0:T(8,128)(2,1)} %collective-permute-done.3, ...), kind=kLoop, calls=%fused_computation.20 | loop fusion | flops 14680064 | bytes 10485792 | tf_op jit(solution)/shard_map/convert_element_type | solution.py:109
  216.2 21.2 %collective-permute-done.7 = bf16[128,4096]{1,0:T(8,128)(2,1)S(1)} collective-permute-done((bf16[128,4096]{1,0:T(8,128)(2,1)S(1)}, bf16[128,4096]{1,0:T(8,128)(2,1)S(1)}, u32[]{:S(2)}, u32[]{:S(2)}) %collective-permute-start.7) | collective-permute-done | bytes 1048608 | tf_op jit(solution)/shard_map/ppermute | solution.py:20
  237.4 1.0 copy.16
  (32 shorter events, 0.7 us)
Async XLA Ops:
  6.5 62.7 %copy-start = (bf16[1,4096,128]{2,1,0:T(8,128)(2,1)S(1)}, bf16[1,4096,128]{2,1,0:T(8,128)(2,1)}, u32[]{:S(2)}) copy-start(bf16[1,4096,128]{2,1,0:T(8,128)(2,1)} %param.10) | copy-start | bytes 3145732
  6.5 54.9 %all-gather.2.cloned.1.call-start = ((), (), s32[]{:S(2)}) async-start(), calls=%async_computation.1 | async-start | bytes 5242880 | tf_op jit(solution)/shard_map/all_gather | solution.py:70
  10.6 199.6 %reduce-scatter.2.cloned.1.call-start = ((), (), s32[]{:S(2)}) async-start(), calls=%async_computation.2 | async-start | bytes 5242880 | tf_op jit(solution)/shard_map/reduce_scatter | solution.py:102
  72.9 7.3 %copy-start.2 = (bf16[1,4096,128]{2,1,0:T(8,128)(2,1)S(1)}, bf16[1,4096,128]{2,1,0:T(8,128)(2,1)}, u32[]{:S(2)}) copy-start(bf16[1,4096,128]{2,1,0:T(8,128)(2,1)} %param.11) | copy-start | bytes 3145732
  80.2 9.9 %slice-start = ((s8[6291456]{0:T(1024)(128)(4,1)}), s8[4194304]{0:T(1024)(128)(4,1)S(1)}, s32[]{:S(2)}) async-start(s8[6291456]{0:T(1024)(128)(4,1)} %bitcast.82), calls=%async_computation.3 | async-start | bytes 8388608
  84.1 6.0 %slice-start.1 = ((s8[6291456]{0:T(1024)(128)(4,1)}), s8[2097152]{0:T(1024)(128)(4,1)S(1)}, s32[]{:S(2)}) async-start(s8[6291456]{0:T(1024)(128)(4,1)} %bitcast.82), calls=%async_computation.4 | async-start | bytes 4194304
  95.3 83.4 %copy-start.5 = (f32[32,8]{0,1:T(8,128)S(1)}, f32[32,8]{0,1:T(8,128)}, u32[]{:S(2)}) copy-start(f32[32,8]{0,1:T(8,128)} %param.13) | copy-start | bytes 3076
  95.3 114.9 %copy-start.1 = (bf16[1,128,4096]{2,1,0:T(8,128)(2,1)S(1)}, bf16[1,128,4096]{2,1,0:T(8,128)(2,1)}, u32[]{:S(2)}) copy-start(bf16[1,128,4096]{2,1,0:T(8,128)(2,1)} %param.7) | copy-start | bytes 3145732
  100.9 27.3 %collective-permute-start = (bf16[128,4096]{1,0:T(8,128)(2,1)S(1)}, bf16[128,4096]{1,0:T(8,128)(2,1)S(1)}, u32[]{:S(2)}, u32[]{:S(2)}) collective-permute-start(bf16[128,4096]{1,0:T(8,128)(2,1)S(1)} %get-tuple-element.13), channel_id=1, source_target_pairs={{0,16},{4,20},{8,24},{12,28},{16,32},{20,36},{24,40},{28,44},{32,4... | collective-permute-start | bytes 3145736 | tf_op jit(solution)/shard_map/ppermute | solution.py:14
  106.1 52.1 %collective-permute-start.1 = (bf16[128,4096]{1,0:T(8,128)(2,1)S(1)}, bf16[128,4096]{1,0:T(8,128)(2,1)S(1)}, u32[]{:S(2)}, u32[]{:S(2)}) collective-permute-start(bf16[128,4096]{1,0:T(8,128)(2,1)S(1)} %get-tuple-element.24), channel_id=1, source_target_pairs={{0,32},{4,36},{8,40},{12,44},{16,48},{20,52},{24,56},{28,60},{32,6... | collective-permute-start | bytes 3145736 | tf_op jit(solution)/shard_map/ppermute | solution.py:14
  109.5 74.3 %collective-permute-start.2 = (bf16[128,4096]{1,0:T(8,128)(2,1)}, bf16[128,4096]{1,0:T(8,128)(2,1)}, u32[]{:S(2)}, u32[]{:S(2)}) collective-permute-start(bf16[128,4096]{1,0:T(8,128)(2,1)} %get-tuple-element.22), channel_id=1, source_target_pairs={{0,48},{4,52},{8,56},{12,60},{16,64},{20,68},{24,72},{28,76},{32,8... | collective-permute-start | bytes 3145736 | tf_op jit(solution)/shard_map/ppermute | solution.py:14
  114.2 69.6 %collective-permute-start.3 = (bf16[128,4096]{1,0:T(8,128)(2,1)}, bf16[128,4096]{1,0:T(8,128)(2,1)}, u32[]{:S(2)}, u32[]{:S(2)}) collective-permute-start(bf16[128,4096]{1,0:T(8,128)(2,1)} %get-tuple-element.20), channel_id=1, source_target_pairs={{0,64},{4,68},{8,72},{12,76},{16,80},{20,84},{24,88},{28,92},{32,9... | collective-permute-start | bytes 3145736 | tf_op jit(solution)/shard_map/ppermute | solution.py:14
  117.0 81.9 %collective-permute-start.4 = (bf16[128,4096]{1,0:T(8,128)(2,1)}, bf16[128,4096]{1,0:T(8,128)(2,1)}, u32[]{:S(2)}, u32[]{:S(2)}) collective-permute-start(bf16[128,4096]{1,0:T(8,128)(2,1)} %get-tuple-element.14), channel_id=1, source_target_pairs={{0,80},{4,84},{8,88},{12,92},{16,96},{20,100},{24,104},{28,108},{3... | collective-permute-start | bytes 3145736 | tf_op jit(solution)/shard_map/ppermute | solution.py:14
  128.2 50.5 %copy-start.3 = (bf16[128,4096]{1,0:T(8,128)(2,1)}, bf16[128,4096]{1,0:T(8,128)(2,1)S(1)}, u32[]{:S(2)}) copy-start(bf16[128,4096]{1,0:T(8,128)(2,1)S(1)} %collective-permute-done) | copy-start | bytes 3145732
  128.2 70.7 %collective-permute-start.5 = (bf16[128,4096]{1,0:T(8,128)(2,1)}, bf16[128,4096]{1,0:T(8,128)(2,1)}, u32[]{:S(2)}, u32[]{:S(2)}) collective-permute-start(bf16[128,4096]{1,0:T(8,128)(2,1)} %get-tuple-element.26), channel_id=1, source_target_pairs={{0,96},{4,100},{8,104},{12,108},{16,112},{20,116},{24,120},{28,124... | collective-permute-start | bytes 3145736 | tf_op jit(solution)/shard_map/ppermute | solution.py:14
  158.2 20.5 %copy-start.4 = (bf16[128,4096]{1,0:T(8,128)(2,1)}, bf16[128,4096]{1,0:T(8,128)(2,1)S(1)}, u32[]{:S(2)}) copy-start(bf16[128,4096]{1,0:T(8,128)(2,1)S(1)} %collective-permute-done.1) | copy-start | bytes 3145732
  158.2 52.1 %collective-permute-start.6 = (bf16[128,4096]{1,0:T(8,128)(2,1)S(1)}, bf16[128,4096]{1,0:T(8,128)(2,1)}, u32[]{:S(2)}, u32[]{:S(2)}) collective-permute-start(bf16[128,4096]{1,0:T(8,128)(2,1)S(1)} %get-tuple-element.25), channel_id=1, source_target_pairs={{0,112},{4,116},{8,120},{12,124},{1,113},{5,117},{9,121},{13,125},... | collective-permute-start | bytes 3145736 | tf_op jit(solution)/shard_map/ppermute | solution.py:14
  216.1 21.3 %collective-permute-start.7 = (bf16[128,4096]{1,0:T(8,128)(2,1)S(1)}, bf16[128,4096]{1,0:T(8,128)(2,1)S(1)}, u32[]{:S(2)}, u32[]{:S(2)}) collective-permute-start(bf16[128,4096]{1,0:T(8,128)(2,1)S(1)} %add_convert_fusion), channel_id=1, source_target_pairs={{124,0},{0,4},{4,8},{8,12},{12,16},{16,20},{20,24},{24,28},{28,32}... | collective-permute-start | bytes 3145736 | tf_op jit(solution)/shard_map/ppermute | solution.py:20
Sparse Core Ops, SparseCore 0:
  10.8 50.6 all-gather.1
  95.5 47.1 reduce-scatter.1
where the time goes:
time: 246 us; the launch traced here: 245 us
  waiting for transfers between devices  107 us (43%)
  starting transfers between devices  68.9 us (28%)
  matrix products  33.5 us (14%)
  between operations  17.8 us (7%)
  other arithmetic  10.1 us (4%)
  local copies, waits for them, and re-layouts  7.55 us (3%)
    ppermute x7, starting transfers between devices, passed_along(): lax.ppermute(value, axis, [(source, source + steps) for source in range(f...  68.8 us
    all_gather x1, waiting for transfers between devices, on_device(): row_piece = lax.all_gather(normed, 'tensor', axis=0, tiled=True)  50.7 us
    ppermute x7, waiting for transfers between devices, passed_along(): lax.ppermute(value, axis, [(source, source + steps) for source in range(f...  35.4 us
    ppermute x1, waiting for transfers between devices, from_behind(): return lax.ppermute(block, axis, route)  21.2 us
    dot_general x1, matrix products, on_device(): jnp.dot(row_piece, query_local, preferred_element_type=jnp.float32)  7.47 us
    sub x1, matrix products, attend(): softmax_weights = jax.nn.softmax(scores, axis=-1).astype(jnp.bfloat16)  7.28 us
    dot_general x1, matrix products, attend(): jnp.einsum('gjts,sgd->tgjd', softmax_weights, value_rows, preferred_eleme...  5.99 us
    convert_element_type x1, other arithmetic, on_device(): (self_coefficient[0] * block_out.astype(jnp.float32) + history_sum).astyp...  5.81 us
  transfers between devices with their start and end apart: 10, of which 5 were waited for; matrix products, arithmetic and copies ran while one was open for 3% of the time, Pallas kernels for 0%

commit v1 on v0

--- a/solution.py
+++ b/solution.py
@@ -67,7 +67,9 @@
     query_local = query_weight[0]
     key_local = key_weight[0]
     value_local = value_weight[0]
-    row_piece = lax.all_gather(normed, "tensor", axis=0, tiled=True)
+    row_piece = jnp.concatenate(
+        lax.all_to_all(jnp.stack([normed] * lax.axis_size("tensor")), "tensor", 0, 0), axis=0
+    )
     query_part = jnp.dot(row_piece, query_local, preferred_element_type=jnp.float32).astype(
         jnp.bfloat16
     )

time: 246 us -> 253 us (1.028)
  starting transfers between devices: 68.9 us -> 72.7 us
    all_gather x1 -> x0, waiting for transfers between devices: 50.7 us -> none  [on_device(): row_piece = lax.all_gather(normed, 'tensor', axis=0, tiled=True)]
    all_to_all x0 -> x1, waiting for transfers between devices: none -> 48.9 us  [on_device(): lax.all_to_all(jnp.stack([normed] * lax.axis_size('tensor')), 'tensor', 0...]
    all_to_all x0 -> x1, starting transfers between devices: none -> 4.83 us  [on_device(): lax.all_to_all(jnp.stack([normed] * lax.axis_size('tensor')), 'tensor', 0...]
    dot_general x1, matrix products: 5.2 us -> 7.79 us  [on_device(): jnp.dot(row_piece, output_local, preferred_element_type=jnp.float32)]
  transfers between devices with their start and end apart: 10 -> 10, of which waited for: 5 -> 5; matrix products, arithmetic and copies ran while one was open for 3% -> 2% of each run, Pallas kernels for 0% -> 0%
where the time goes in v1:
time: 253 us
  waiting for transfers between devices  107 us (42%)
  starting transfers between devices  72.7 us (29%)
  matrix products  35.8 us (14%)
  between operations  18.1 us (7%)
  local copies, waits for them, and re-layouts  9.69 us (4%)
  other arithmetic  9.31 us (4%)
    ppermute x7, starting transfers between devices, passed_along(): lax.ppermute(value, axis, [(source, source + steps) for source in range(f...  67.8 us
    all_to_all x1, waiting for transfers between devices, on_device(): lax.all_to_all(jnp.stack([normed] * lax.axis_size('tensor')), 'tensor', 0...  48.9 us
    ppermute x7, waiting for transfers between devices, passed_along(): lax.ppermute(value, axis, [(source, source + steps) for source in range(f...  34.8 us
    ppermute x1, waiting for transfers between devices, from_behind(): return lax.ppermute(block, axis, route)  23.2 us
    dot_general x1, matrix products, on_device(): jnp.dot(row_piece, output_local, preferred_element_type=jnp.float32)  7.79 us
    dot_general x1, matrix products, on_device(): jnp.dot(row_piece, query_local, preferred_element_type=jnp.float32)  7.46 us
    sub x1, matrix products, attend(): softmax_weights = jax.nn.softmax(scores, axis=-1).astype(jnp.bfloat16)  7.27 us
    convert_element_type x1, other arithmetic, on_device(): (self_coefficient[0] * block_out.astype(jnp.float32) + history_sum).astyp...  6.01 us
  transfers between devices with their start and end apart: 10, of which 5 were waited for; matrix products, arithmetic and copies ran while one was open for 2% of the time, Pallas kernels for 0%

profile of v1, /device:TPU:0, one launch (start us, length us, event | category | flops | bytes accessed | tf_op | source)
XLA Modules:
  0.0 252.5 jit_solution(7688385494084288941)
XLA Ops:
  6.5 1.6 fusion.15
  8.2 1.5 fusion.24
  9.6 2.5 stack.10
  12.1 4.8 %all-to-all-start = ((bf16[4,128,4096]{2,1,0:T(8,128)(2,1)}), bf16[4,128,4096]{2,1,0:T(8,128)(2,1)}, u32[]{:S(2)}, u32[]{:S(2)}) async-start(bf16[4,128,4096]{2,1,0:T(8,128)(2,1)} %stack.10), calls=%async_computation | async-start | bytes 8388608 | tf_op jit(solution)/shard_map/all_to_all | solution.py:71
  17.1 48.9 %all-to-all-done = bf16[4,128,4096]{2,1,0:T(8,128)(2,1)} async-done(((bf16[4,128,4096]{2,1,0:T(8,128)(2,1)}), bf16[4,128,4096]{2,1,0:T(8,128)(2,1)}, u32[]{:S(2)}, u32[]{:S(2)}) %all-to-all-start) | async-done | bytes 4194336 | tf_op jit(solution)/shard_map/all_to_all | solution.py:71
  66.0 7.5 %fusion.21 = bf16[512,768]{1,0:T(8,128)(2,1)S(1)} fusion(bf16[512,4096]{1,0:T(8,128)(2,1)} %bitcast.3, bf16[1,4096,768]{2,1,0:T(8,128)(2,1)} %param.9), kind=kOutput, calls=%fused_computation.24 | convolution fusion | flops 3221618688 | bytes 11272192 | tf_op jit(solution)/shard_map/dot_general | solution.py:73
  73.8 3.8 %convolution_convert_fusion = bf16[512,128]{0,1:T(8,128)(2,1)S(1)} fusion(bf16[512,4096]{1,0:T(8,128)(2,1)} %bitcast.3, bf16[1,4096,128]{2,1,0:T(8,128)(2,1)S(1)} %copy-done), kind=kOutput, calls=%fused_computation.25 | convolution fusion | flops 536936448 | bytes 5373952 | tf_op jit(solution)/shard_map/dot_general | solution.py:76
  77.6 3.7 %convolution_convert_fusion.1 = bf16[512,128]{0,1:T(8,128)(2,1)S(1)} fusion(bf16[512,4096]{1,0:T(8,128)(2,1)} %bitcast.3, bf16[1,4096,128]{2,1,0:T(8,128)(2,1)S(1)} %copy-done.3), kind=kOutput, calls=%fused_computation.26 | convolution fusion | flops 536936448 | bytes 5373952 | tf_op jit(solution)/shard_map/dot_general | solution.py:79
  81.3 7.3 %fusion.30 = (f32[2,6,512]{2,1,0:T(8,128)S(1)}, f32[2,6,512,512]{2,3,1,0:T(8,128)}) fusion(pred[512,512]{0,1:T(8,128)(4,1)S(1)} %iota_compare_fusion, bf16[512,2,64,1]{0,2,3,1:T(8,128)(2,1)S(1)} %bitcast.91, bf16[512,2,6,64]{0,3,2,1:T(8,128)(2,1)S(1)} %bitcast.89), kind=kOutput, calls=%fused_computation.44 | convolution fusion | flops 415236608 | bytes 13787136 | tf_op jit(solution)/shard_map/while/body/eval_jaxpr/sub | solution.py:41
  88.6 5.8 %fusion.20 = bf16[2,64,6,512]{3,1,2,0:T(8,128)(2,1)S(1)} fusion(bf16[512,2,64,1]{0,2,3,1:T(8,128)(2,1)S(1)} %bitcast.90, f32[2,6,512,512]{2,3,1,0:T(8,128)} %get-tuple-element.36, f32[2,6,512]{2,1,0:T(8,128)S(1)} %get-tuple-element.35), kind=kOutput, calls=%fused_computation.23 | convolution fusion | flops 409337856 | bytes 13524992 | tf_op jit(solution)/shard_map/while/body/eval_jaxpr/gjts,sgd->tgjd/dot_general | solution.py:42
  94.4 7.8 %fusion.10 = bf16[512,4096]{1,0:T(8,128)(2,1)} fusion(bf16[512,768]{0,1:T(8,128)(2,1)S(1)} %bitcast.92, bf16[1,768,4096]{2,1,0:T(8,128)(2,1)} %param.12), kind=kOutput, calls=%fused_computation.13 | convolution fusion | flops 3223322624 | bytes 11272192 | tf_op jit(solution)/shard_map/dot_general | solution.py:101
  102.2 5.2 %slice_bitcast_fusion.6 = (bf16[128,4096]{1,0:T(8,128)(2,1)S(1)}, bf16[128,4096]{1,0:T(8,128)(2,1)}, bf16[128,4096]{1,0:T(8,128)(2,1)}, bf16[128,4096]{1,0:T(8,1...) fusion(bf16[1,7,128,4096]{3,2,1,0:T(8,128)(2,1)} %param.8), kind=kLoop, calls=%fused_computation.36 | loop fusion | bytes 14680064 | tf_op jit(solution)/shard_map/squeeze | solution.py:58
  107.4 6.0 %collective-permute-start = (bf16[128,4096]{1,0:T(8,128)(2,1)S(1)}, bf16[128,4096]{1,0:T(8,128)(2,1)S(1)}, u32[]{:S(2)}, u32[]{:S(2)}) collective-permute-start(bf16[128,4096]{1,0:T(8,128)(2,1)S(1)} %get-tuple-element.13), channel_id=1, source_target_pairs={{0,16},{4,20},{8,24},{12,28},{16,32},{20,36},{24,40},{28,44},{32,4... | collective-permute-start | bytes 3145736 | tf_op jit(solution)/shard_map/ppermute | solution.py:14
  113.5 3.7 %collective-permute-start.1 = (bf16[128,4096]{1,0:T(8,128)(2,1)S(1)}, bf16[128,4096]{1,0:T(8,128)(2,1)S(1)}, u32[]{:S(2)}, u32[]{:S(2)}) collective-permute-start(bf16[128,4096]{1,0:T(8,128)(2,1)S(1)} %get-tuple-element.24), channel_id=1, source_target_pairs={{0,32},{4,36},{8,40},{12,44},{16,48},{20,52},{24,56},{28,60},{32,6... | collective-permute-start | bytes 3145736 | tf_op jit(solution)/shard_map/ppermute | solution.py:14
  117.2 4.2 %collective-permute-start.2 = (bf16[128,4096]{1,0:T(8,128)(2,1)}, bf16[128,4096]{1,0:T(8,128)(2,1)}, u32[]{:S(2)}, u32[]{:S(2)}) collective-permute-start(bf16[128,4096]{1,0:T(8,128)(2,1)} %get-tuple-element.22), channel_id=1, source_target_pairs={{0,48},{4,52},{8,56},{12,60},{16,64},{20,68},{24,72},{28,76},{32,8... | collective-permute-start | bytes 3145736 | tf_op jit(solution)/shard_map/ppermute | solution.py:14
  121.3 3.5 %collective-permute-start.3 = (bf16[128,4096]{1,0:T(8,128)(2,1)}, bf16[128,4096]{1,0:T(8,128)(2,1)}, u32[]{:S(2)}, u32[]{:S(2)}) collective-permute-start(bf16[128,4096]{1,0:T(8,128)(2,1)} %get-tuple-element.20), channel_id=1, source_target_pairs={{0,64},{4,68},{8,72},{12,76},{16,80},{20,84},{24,88},{28,92},{32,9... | collective-permute-start | bytes 3145736 | tf_op jit(solution)/shard_map/ppermute | solution.py:14
  124.9 2.3 collective-permute-start.4
  127.2 7.8 %collective-permute-done = bf16[128,4096]{1,0:T(8,128)(2,1)S(1)} collective-permute-done((bf16[128,4096]{1,0:T(8,128)(2,1)S(1)}, bf16[128,4096]{1,0:T(8,128)(2,1)S(1)}, u32[]{:S(2)}, u32[]{:S(2)}) %collective-permute-start) | collective-permute-done | bytes 1048608 | tf_op jit(solution)/shard_map/ppermute | solution.py:14
  135.0 28.7 %collective-permute-start.5 = (bf16[128,4096]{1,0:T(8,128)(2,1)S(1)}, bf16[128,4096]{1,0:T(8,128)(2,1)}, u32[]{:S(2)}, u32[]{:S(2)}) collective-permute-start(bf16[128,4096]{1,0:T(8,128)(2,1)S(1)} %get-tuple-element.26), channel_id=1, source_target_pairs={{0,96},{4,100},{8,104},{12,108},{16,112},{20,116},{24,120},{28,124... | collective-permute-start | bytes 3145736 | tf_op jit(solution)/shard_map/ppermute | solution.py:14
  163.7 19.3 %collective-permute-start.6 = (bf16[128,4096]{1,0:T(8,128)(2,1)S(1)}, bf16[128,4096]{1,0:T(8,128)(2,1)}, u32[]{:S(2)}, u32[]{:S(2)}) collective-permute-start(bf16[128,4096]{1,0:T(8,128)(2,1)S(1)} %get-tuple-element.25), channel_id=1, source_target_pairs={{0,112},{4,116},{8,120},{12,124},{1,113},{5,117},{9,121},{13,125},... | collective-permute-start | bytes 3145736 | tf_op jit(solution)/shard_map/ppermute | solution.py:14
  188.4 17.4 %collective-permute-done.4 = bf16[128,4096]{1,0:T(8,128)(2,1)} collective-permute-done((bf16[128,4096]{1,0:T(8,128)(2,1)}, bf16[128,4096]{1,0:T(8,128)(2,1)}, u32[]{:S(2)}, u32[]{:S(2)}) %collective-permute-start.4) | collective-permute-done | bytes 1048608 | tf_op jit(solution)/shard_map/ppermute | solution.py:14
  205.8 9.6 %collective-permute-done.6 = bf16[128,4096]{1,0:T(8,128)(2,1)} collective-permute-done((bf16[128,4096]{1,0:T(8,128)(2,1)S(1)}, bf16[128,4096]{1,0:T(8,128)(2,1)}, u32[]{:S(2)}, u32[]{:S(2)}) %collective-permute-start.6) | collective-permute-done | bytes 1048608 | tf_op jit(solution)/shard_map/ppermute | solution.py:14
  215.4 6.0 %add_convert_fusion = bf16[128,4096]{1,0:T(8,128)(2,1)S(1)} fusion(bf16[128,4096]{1,0:T(8,128)(2,1)} %collective-permute-done.6, bf16[128,4096]{1,0:T(8,128)(2,1)} %collective-permute-done.5, bf16[128,4096]{1,0:T(8,128)(2,1)} %collective-permute-done.4, bf16[128,4096]{1,0:T(8,128)(2,1)} %collective-permute-done.3, ...), kind=kLoop, calls=%fused_computation.21 | loop fusion | flops 14680064 | bytes 10485792 | tf_op jit(solution)/shard_map/convert_element_type | solution.py:111
  221.5 23.2 %collective-permute-done.7 = bf16[128,4096]{1,0:T(8,128)(2,1)S(1)} collective-permute-done((bf16[128,4096]{1,0:T(8,128)(2,1)S(1)}, bf16[128,4096]{1,0:T(8,128)(2,1)S(1)}, u32[]{:S(2)}, u32[]{:S(2)}) %collective-permute-start.7) | collective-permute-done | bytes 1048608 | tf_op jit(solution)/shard_map/ppermute | solution.py:20
  (29 shorter events, 2.3 us)
Async XLA Ops:
  6.5 67.3 %copy-start = (bf16[1,4096,128]{2,1,0:T(8,128)(2,1)S(1)}, bf16[1,4096,128]{2,1,0:T(8,128)(2,1)}, u32[]{:S(2)}) copy-start(bf16[1,4096,128]{2,1,0:T(8,128)(2,1)} %param.10) | copy-start | bytes 3145732
  12.1 53.9 %all-to-all-start = ((bf16[4,128,4096]{2,1,0:T(8,128)(2,1)}), bf16[4,128,4096]{2,1,0:T(8,128)(2,1)}, u32[]{:S(2)}, u32[]{:S(2)}) async-start(bf16[4,128,4096]{2,1,0:T(8,128)(2,1)} %stack.10), calls=%async_computation | async-start | bytes 8388608 | tf_op jit(solution)/shard_map/all_to_all | solution.py:71
  17.0 198.4 %reduce-scatter.2.cloned.1.call-start = ((), (), s32[]{:S(2)}) async-start(), calls=%async_computation.2 | async-start | bytes 5242880 | tf_op jit(solution)/shard_map/reduce_scatter | solution.py:104
  73.8 3.8 %copy-start.3 = (bf16[1,4096,128]{2,1,0:T(8,128)(2,1)S(1)}, bf16[1,4096,128]{2,1,0:T(8,128)(2,1)}, u32[]{:S(2)}) copy-start(bf16[1,4096,128]{2,1,0:T(8,128)(2,1)} %param.11) | copy-start | bytes 3145732
  102.2 80.8 %copy-start.6 = (f32[32,8]{0,1:T(8,128)S(1)}, f32[32,8]{0,1:T(8,128)}, u32[]{:S(2)}) copy-start(f32[32,8]{0,1:T(8,128)} %param.13) | copy-start | bytes 3076
  102.2 113.2 %copy-start.2 = (bf16[1,128,4096]{2,1,0:T(8,128)(2,1)S(1)}, bf16[1,128,4096]{2,1,0:T(8,128)(2,1)}, u32[]{:S(2)}) copy-start(bf16[1,128,4096]{2,1,0:T(8,128)(2,1)} %param.7) | copy-start | bytes 3145732
  107.4 27.5 %collective-permute-start = (bf16[128,4096]{1,0:T(8,128)(2,1)S(1)}, bf16[128,4096]{1,0:T(8,128)(2,1)S(1)}, u32[]{:S(2)}, u32[]{:S(2)}) collective-permute-start(bf16[128,4096]{1,0:T(8,128)(2,1)S(1)} %get-tuple-element.13), channel_id=1, source_target_pairs={{0,16},{4,20},{8,24},{12,28},{16,32},{20,36},{24,40},{28,44},{32,4... | collective-permute-start | bytes 3145736 | tf_op jit(solution)/shard_map/ppermute | solution.py:14
  113.5 50.2 %collective-permute-start.1 = (bf16[128,4096]{1,0:T(8,128)(2,1)S(1)}, bf16[128,4096]{1,0:T(8,128)(2,1)S(1)}, u32[]{:S(2)}, u32[]{:S(2)}) collective-permute-start(bf16[128,4096]{1,0:T(8,128)(2,1)S(1)} %get-tuple-element.24), channel_id=1, source_target_pairs={{0,32},{4,36},{8,40},{12,44},{16,48},{20,52},{24,56},{28,60},{32,6... | collective-permute-start | bytes 3145736 | tf_op jit(solution)/shard_map/ppermute | solution.py:14
  117.2 71.2 %collective-permute-start.2 = (bf16[128,4096]{1,0:T(8,128)(2,1)}, bf16[128,4096]{1,0:T(8,128)(2,1)}, u32[]{:S(2)}, u32[]{:S(2)}) collective-permute-start(bf16[128,4096]{1,0:T(8,128)(2,1)} %get-tuple-element.22), channel_id=1, source_target_pairs={{0,48},{4,52},{8,56},{12,60},{16,64},{20,68},{24,72},{28,76},{32,8... | collective-permute-start | bytes 3145736 | tf_op jit(solution)/shard_map/ppermute | solution.py:14
  121.3 67.1 %collective-permute-start.3 = (bf16[128,4096]{1,0:T(8,128)(2,1)}, bf16[128,4096]{1,0:T(8,128)(2,1)}, u32[]{:S(2)}, u32[]{:S(2)}) collective-permute-start(bf16[128,4096]{1,0:T(8,128)(2,1)} %get-tuple-element.20), channel_id=1, source_target_pairs={{0,64},{4,68},{8,72},{12,76},{16,80},{20,84},{24,88},{28,92},{32,9... | collective-permute-start | bytes 3145736 | tf_op jit(solution)/shard_map/ppermute | solution.py:14
  124.9 80.9 %collective-permute-start.4 = (bf16[128,4096]{1,0:T(8,128)(2,1)}, bf16[128,4096]{1,0:T(8,128)(2,1)}, u32[]{:S(2)}, u32[]{:S(2)}) collective-permute-start(bf16[128,4096]{1,0:T(8,128)(2,1)} %get-tuple-element.14), channel_id=1, source_target_pairs={{0,80},{4,84},{8,88},{12,92},{16,96},{20,100},{24,104},{28,108},{3... | collective-permute-start | bytes 3145736 | tf_op jit(solution)/shard_map/ppermute | solution.py:14
  135.0 48.0 %copy-start.4 = (bf16[128,4096]{1,0:T(8,128)(2,1)}, bf16[128,4096]{1,0:T(8,128)(2,1)S(1)}, u32[]{:S(2)}) copy-start(bf16[128,4096]{1,0:T(8,128)(2,1)S(1)} %collective-permute-done) | copy-start | bytes 3145732
  135.0 70.8 %collective-permute-start.5 = (bf16[128,4096]{1,0:T(8,128)(2,1)S(1)}, bf16[128,4096]{1,0:T(8,128)(2,1)}, u32[]{:S(2)}, u32[]{:S(2)}) collective-permute-start(bf16[128,4096]{1,0:T(8,128)(2,1)S(1)} %get-tuple-element.26), channel_id=1, source_target_pairs={{0,96},{4,100},{8,104},{12,108},{16,112},{20,116},{24,120},{28,124... | collective-permute-start | bytes 3145736 | tf_op jit(solution)/shard_map/ppermute | solution.py:14
  163.7 19.3 %copy-start.5 = (bf16[128,4096]{1,0:T(8,128)(2,1)}, bf16[128,4096]{1,0:T(8,128)(2,1)S(1)}, u32[]{:S(2)}) copy-start(bf16[128,4096]{1,0:T(8,128)(2,1)S(1)} %collective-permute-done.1) | copy-start | bytes 3145732
  163.7 51.7 %collective-permute-start.6 = (bf16[128,4096]{1,0:T(8,128)(2,1)S(1)}, bf16[128,4096]{1,0:T(8,128)(2,1)}, u32[]{:S(2)}, u32[]{:S(2)}) collective-permute-start(bf16[128,4096]{1,0:T(8,128)(2,1)S(1)} %get-tuple-element.25), channel_id=1, source_target_pairs={{0,112},{4,116},{8,120},{12,124},{1,113},{5,117},{9,121},{13,125},... | collective-permute-start | bytes 3145736 | tf_op jit(solution)/shard_map/ppermute | solution.py:14
  215.4 30.3 %copy-start.1 = (bf16[1,4096,128]{2,1,0:T(8,128)(2,1)S(1)}, bf16[1,4096,128]{2,1,0:T(8,128)(2,1)}, u32[]{:S(2)}) copy-start(bf16[1,4096,128]{2,1,0:T(8,128)(2,1)} %param.10) | copy-start | bytes 3145732
  221.4 23.3 %collective-permute-start.7 = (bf16[128,4096]{1,0:T(8,128)(2,1)S(1)}, bf16[128,4096]{1,0:T(8,128)(2,1)S(1)}, u32[]{:S(2)}, u32[]{:S(2)}) collective-permute-start(bf16[128,4096]{1,0:T(8,128)(2,1)S(1)} %add_convert_fusion), channel_id=1, source_target_pairs={{124,0},{0,4},{4,8},{8,12},{12,16},{16,20},{20,24},{24,28},{28,32}... | collective-permute-start | bytes 3145736 | tf_op jit(solution)/shard_map/ppermute | solution.py:20
Sparse Core Ops, SparseCore 0:
  102.3 47.4 reduce-scatter.1
